TPU v7x, 32 devices: a whole 2x2x4 slice. The times are simulated.
32 devices in a mesh: seq: 8 (over z, y), mp: 4 (over x, core).
Axes of the slice: x: 2, y: 2, z: 4, core: 2. Of those that a mesh axis runs over, the one named last changes fastest.
Arguments:
- hidden_in: bfloat16 [2, 1024, 2048], P(None, 'seq'), may hold values from -6 to 6
- attn_gain: float32 [2048], replicated, may hold values from 0.1 to 1.9
- q_weight: bfloat16 [2048, 2048], P(None, 'mp'), may hold values from -0.125 to 0.125
- q_bias: float32 [2048], P('mp'), may hold values from -60 to 60
- k_weight: bfloat16 [2048, 256], replicated, may hold values from -0.125 to 0.125
- k_bias: float32 [256], replicated, may hold values from -60 to 60
- v_weight: bfloat16 [2048, 256], replicated, may hold values from -0.125 to 0.125
- v_bias: float32 [256], replicated, may hold values from -3 to 3
- o_weight: bfloat16 [2048, 2048], P('mp'), may hold values from -0.125 to 0.125
- mlp_gain: float32 [2048], replicated, may hold values from 0.1 to 1.9
- gate_weight: bfloat16 [2048, 5632], P('seq', 'mp'), may hold values from -0.125 to 0.125
- up_weight: bfloat16 [2048, 5632], P('seq', 'mp'), may hold values from -0.125 to 0.125
- down_weight: bfloat16 [2048, 5632], P('seq', 'mp'), may hold values from -0.078125 to 0.078125
- lengths: int32 [2], replicated, may hold values from 512 to 1024
Outputs:
- layer_out: bfloat16 [2, 1024, 2048], P(None, 'seq', 'mp')
- influence: float32 [2, 1024], P(None, 'seq')
- score: float32 [2], replicated
Inputs may be any that keep to these rules, and one draw needn't show every extreme that they name: `lengths`: tokens at positions 512 and later may be invalid.
All inputs are finite; a program needn't handle non-finite values.
Results may differ from a plain program's by a relative error of at most 0.02.
The roundings to bfloat16 on the way count: a program that leaves them out, or rounds other values in their place, can miss the bound.
Values may be sent and summed in bfloat16 or wider, within the bound.
A program may use at most 192 MiB of HBM per device.

v0:
```python
import jax
import jax.numpy as jnp
from jax import lax
from jax.sharding import PartitionSpec as P

HEADS = 16
KV_HEADS = 2
HEAD = 128
rope_base = 1000000.0
norm_eps = 1e-06
masked_score = -1e30


def rms_scale(values, gain):
    widened = values.astype(jnp.float32)
    factor = lax.rsqrt(jnp.mean(widened * widened, axis=-1, keepdims=True) + norm_eps)
    return (widened * factor * gain).astype(jnp.bfloat16)


def rotate(values, positions):
    head_width = values.shape[-1]
    half_width = head_width // 2
    inv_freq = rope_base ** (-(jnp.arange(half_width, dtype=jnp.float32) * 2.0) / head_width)
    angles = positions.astype(jnp.float32)[:, None] * inv_freq[None, :]
    angles = jnp.concatenate([angles, angles], axis=-1)
    first_part = values[..., :half_width]
    second_part = values[..., half_width:]
    turned = jnp.concatenate([-second_part, first_part], axis=-1)
    return values * jnp.cos(angles) + turned * jnp.sin(angles)


def attend_update(state, queries, first_pos, key_piece, value_piece):
    run_max, run_sum, run_acc = state
    score_scale = queries.shape[-1] ** (-0.5)
    query_pos = first_pos + jnp.arange(queries.shape[2], dtype=jnp.int32)
    key_pos = jnp.arange(key_piece.shape[1], dtype=jnp.int32)
    scores = (
        jnp.einsum("shqd,skd->shqk", queries, key_piece, preferred_element_type=jnp.float32)
        * score_scale
    )
    allowed = key_pos[None, :] <= query_pos[:, None]
    scores = jnp.where(allowed, scores, masked_score)
    new_max = jnp.maximum(run_max, jnp.max(scores, axis=-1))
    weights = jnp.where(allowed, jnp.exp(scores - new_max[..., None]), 0.0)
    new_sum = jnp.sum(weights, axis=-1)
    mixed = jnp.einsum(
        "shqk,skd->shqd",
        weights.astype(jnp.bfloat16),
        value_piece,
        preferred_element_type=jnp.float32,
    )
    return (new_max, new_sum, mixed)


def local(
    hidden_in,
    attn_gain,
    q_weight,
    q_bias,
    k_weight,
    k_bias,
    v_weight,
    v_bias,
    o_weight,
    mlp_gain,
    gate_weight,
    up_weight,
    down_weight,
    lengths,
):
    seqs_n, tok_n, width = hidden_in.shape
    seq_rank = lax.axis_index("seq")
    mp_devices = lax.axis_size("mp")
    mp_rank = lax.axis_index("mp")
    heads_here = q_weight.shape[1] // HEAD
    group_size = HEADS // KV_HEADS
    kv_index = mp_rank * heads_here // group_size
    flat_in = hidden_in.reshape(seqs_n * tok_n, width)
    normed = rms_scale(flat_in, attn_gain)
    query_all = jnp.dot(normed, q_weight, preferred_element_type=jnp.float32) + q_bias
    key_cols = lax.dynamic_slice_in_dim(k_weight, kv_index * HEAD, HEAD, 1)
    value_cols = lax.dynamic_slice_in_dim(v_weight, kv_index * HEAD, HEAD, 1)
    key_shift = lax.dynamic_slice_in_dim(k_bias, kv_index * HEAD, HEAD, 0)
    value_shift = lax.dynamic_slice_in_dim(v_bias, kv_index * HEAD, HEAD, 0)
    key_all = jnp.dot(normed, key_cols, preferred_element_type=jnp.float32) + key_shift
    value_rows = (
        jnp.dot(normed, value_cols, preferred_element_type=jnp.float32) + value_shift
    ).astype(jnp.bfloat16)
    positions = seq_rank * tok_n + jnp.arange(tok_n, dtype=jnp.int32)
    rotated_q = rotate(
        query_all.reshape(seqs_n, tok_n, heads_here, HEAD).transpose(0, 2, 1, 3), positions
    ).astype(jnp.bfloat16)
    rotated_k = rotate(key_all.reshape(seqs_n, tok_n, HEAD), positions).astype(jnp.bfloat16)
    value_rows = value_rows.reshape(seqs_n, tok_n, HEAD)
    query_sets = ((rotated_q, seq_rank * tok_n),)
    initial = tuple(
        (
            (
                jnp.full(entry[0].shape[:3], masked_score, jnp.float32),
                jnp.zeros(entry[0].shape[:3], jnp.float32),
                jnp.zeros(entry[0].shape, jnp.float32),
            )
            for entry in query_sets
        )
    )
    key_start = jnp.int32(0)
    key_piece = lax.all_gather(rotated_k, "seq", axis=1, tiled=True)
    value_piece = lax.all_gather(value_rows, "seq", axis=1, tiled=True)
    updated = []
    for state, query_entry in zip(initial, query_sets):
        queries, first_pos = query_entry
        last_pos = first_pos + queries.shape[2] - 1

        def run_update(current):
            return attend_update(current, queries, first_pos, key_piece, value_piece)

        def keep_state(current):
            return current

        updated.append(lax.cond(key_start <= last_pos, run_update, keep_state, state))
    results = tuple(updated)
    finished = [(entry[2] / entry[1][..., None]).astype(jnp.bfloat16) for entry in results]
    attn = finished[0]
    attn = attn.transpose(0, 2, 1, 3).reshape(seqs_n * tok_n, heads_here * HEAD)
    projected = jnp.dot(attn, o_weight, preferred_element_type=jnp.float32)
    quarter = width // mp_devices
    own_in = lax.dynamic_slice_in_dim(flat_in, mp_rank * quarter, quarter, 1)
    summed = lax.psum(projected.astype(jnp.bfloat16), "mp").astype(jnp.float32)
    residual = (flat_in.astype(jnp.float32) + summed).astype(jnp.bfloat16)
    resid_part = lax.dynamic_slice_in_dim(residual, mp_rank * quarter, quarter, 1)
    mlp_in = rms_scale(residual, mlp_gain)
    gate_sum = jnp.dot(
        mlp_in,
        lax.all_gather(gate_weight, "seq", axis=0, tiled=True),
        preferred_element_type=jnp.float32,
    )
    up_sum = jnp.dot(
        mlp_in,
        lax.all_gather(up_weight, "seq", axis=0, tiled=True),
        preferred_element_type=jnp.float32,
    )
    activated = (jax.nn.silu(gate_sum) * up_sum).astype(jnp.bfloat16)
    down_part = lax.dot_general(
        activated,
        lax.all_gather(down_weight, "seq", axis=0, tiled=True),
        (((1,), (1,)), ((), ())),
        preferred_element_type=jnp.float32,
    )
    mlp_share = lax.psum_scatter(
        down_part.astype(jnp.bfloat16), "mp", scatter_dimension=1, tiled=True
    ).astype(jnp.float32)
    layer_part = (resid_part.astype(jnp.float32) + mlp_share).astype(jnp.bfloat16)
    in_share = own_in.astype(jnp.float32)
    out_share = layer_part.astype(jnp.float32)
    cross_part = jnp.sum(in_share * out_share, axis=-1).reshape(seqs_n, tok_n)
    out_part = jnp.sum(out_share * out_share, axis=-1).reshape(seqs_n, tok_n)
    cross, out_norm = lax.psum((cross_part, out_part), "mp")
    in_wide = flat_in.astype(jnp.float32)
    in_norm = jnp.sum(in_wide * in_wide, axis=-1).reshape(seqs_n, tok_n)
    cosine = cross / jnp.sqrt((in_norm + norm_eps) * (out_norm + norm_eps))
    valid = positions[None, :] < lengths[:, None]
    influence = jnp.where(valid, 1.0 - cosine, 0.0)
    seq_total = lax.psum(jnp.sum(influence, axis=1), "seq")
    score = seq_total / lengths.astype(jnp.float32)
    return (layer_part.reshape(seqs_n, tok_n, quarter), influence, score)


def solution(mesh):
    placed = (
        P(None, "seq", None),
        P(),
        P(None, "mp"),
        P("mp"),
        P(),
        P(),
        P(),
        P(),
        P("mp", None),
        P(),
        P("seq", "mp"),
        P("seq", "mp"),
        P("seq", "mp"),
        P(),
    )
    return jax.shard_map(
        local,
        mesh=mesh,
        in_specs=placed,
        out_specs=(P(None, "seq", "mp"), P(None, "seq"), P()),
        check_vma=False,
    )
```

profile of v0, /device:TPU:0, one launch (start us, length us, event | category | flops | bytes accessed | tf_op | source)
XLA Modules:
  0.0 447.5 jit_solution(1680391220494171423)
XLA Ops:
  8.0 0.0 all-reduce.3.cloned.1.call-start
  8.1 1.6 multiply_reduce_fusion
  9.8 0.8 dynamic_slice.19
  10.6 1.5 fusion.14
  12.2 0.4 convolution_add_fusion.2
  12.6 0.7 slice_negate_fusion.1
  13.3 0.1 broadcast_multiply_fusion
  13.4 0.3 fusion.36
  13.8 1.2 fusion.34
  15.0 35.3 %all_gather.15 = bf16[2,1024,128]{2,1,0:T(8,128)(2,1)} all-gather(bf16[2,128,128]{2,1,0:T(8,128)(2,1)S(1)} %fusion.34), channel_id=1, replica_groups=mesh['seq'=8,'mp'=4] {'seq'}, dimensions={1}, use_global_device_ids=true | all-gather | bytes 589824 | tf_op jit(solution)/shard_map/all_gather | solution.py:107
  50.2 0.1 dynamic_slice.21
  50.3 1.5 fusion.19
  51.8 33.2 %all_gather.16 = bf16[2,1024,128]{2,1,0:T(8,128)(2,1)} all-gather(bf16[2,128,128]{2,1,0:T(8,128)(2,1)S(1)} %bitcast.49), channel_id=1, replica_groups=mesh['seq'=8,'mp'=4] {'seq'}, dimensions={1}, use_global_device_ids=true | all-gather | bytes 589824 | tf_op jit(solution)/shard_map/all_gather | solution.py:108
  85.0 1.5 convolution_add_fusion
  86.5 1.2 reshape.194
  87.8 1.2 slice_negate_fusion
  88.9 1.4 fusion.23
  90.4 3.7 conditional.1
  90.4 0.1 iota_compare_fusion
  90.5 0.9 fusion
  91.5 0.1 copy-done.3
  91.6 1.1 fusion.3
  92.7 1.3 fusion.2
  94.0 0.2 fusion.32
  94.3 0.2 copy.19
  94.5 1.7 convolution_convert_fusion
  96.2 0.0 all-reduce.3.cloned.1.call-update
  96.2 0.0 all-gather.4.cloned.1.call-start
  96.2 0.5 all-gather.4.cloned.1.call-update
  96.8 0.0 all-gather.6.cloned.1.call-start
  96.8 0.5 all-gather.6.cloned.1.call-update
  97.4 0.0 all-gather.8.cloned.1.call-start
  97.4 0.5 all-gather.8.cloned.1.call-update
  97.9 0.2 reduce-scatter.2.cloned.1.call-start
  98.2 35.9 %all-reduce.3.cloned.1.call-done = bf16[256,2048]{1,0:T(8,128)(2,1)} async-done(((bf16[256,2048]{1,0:T(8,128)(2,1)}), bf16[256,2048]{1,0:T(8,128)(2,1)}) %all-reduce.3.cloned.1.call-update) | async-done | bytes 1048592 | tf_op jit(solution)/shard_map/psum | solution.py:128
  134.1 2.6 fusion.16
  136.7 55.5 %all-gather.4.cloned.1.call-done = bf16[2048,1408]{1,0:T(8,128)(2,1)} async-done(((bf16[256,1408]{1,0:T(8,128)(2,1)}), bf16[2048,1408]{1,0:T(8,128)(2,1)}) %all-gather.4.cloned.1.call-update) | async-done | bytes 5767184 | tf_op jit(solution)/shard_map/all_gather | solution.py:134
  192.2 6.0 %fusion.28 = f32[256,1408]{1,0:T(8,128)} fusion(bf16[2048,1408]{1,0:T(8,128)(2,1)} %all-gather.4.cloned.1.call-done, bf16[256,2048]{1,0:T(8,128)(2,1)} %get-tuple-element.27, f32[2048]{0:T(1024)S(1)} %copy-done.7, f32[256]{0:T(256)S(1)} %add_rsqrt_fusion), kind=kOutput, calls=%fused_computation.48 | convolution fusion | flops 1478492160 | bytes 8266752 | tf_op jit(solution)/shard_map/dot_general | solution.py:132
  198.2 86.4 %all-gather.6.cloned.1.call-done = bf16[2048,1408]{1,0:T(8,128)(2,1)} async-done(((bf16[256,1408]{1,0:T(8,128)(2,1)}), bf16[2048,1408]{1,0:T(8,128)(2,1)}) %all-gather.6.cloned.1.call-update) | async-done | bytes 5767184 | tf_op jit(solution)/shard_map/all_gather | solution.py:139
  284.6 92.4 %all-gather.8.cloned.1.call-done = bf16[2048,1408]{1,0:T(8,128)(2,1)} async-done(((bf16[256,1408]{1,0:T(8,128)(2,1)}), bf16[2048,1408]{1,0:T(8,128)(2,1)}) %all-gather.8.cloned.1.call-update) | async-done | bytes 5767184 | tf_op jit(solution)/shard_map/all_gather | solution.py:145
  376.9 9.5 %convolution_convert_fusion.1 = bf16[256,2048]{1,0:T(8,128)(2,1)} fusion(bf16[2048,1408]{1,0:T(8,128)(2,1)} %all-gather.8.cloned.1.call-done, bf16[2048,1408]{1,0:T(8,128)(2,1)} %all-gather.6.cloned.1.call-done, f32[256,1408]{1,0:T(8,128)} %fusion.28, bf16[256,2048]{1,0:T(8,128)(2,1)} %get-tuple-element.27, f32[2048]{0:T(1024)S(1)} %copy-done.7, ...), kind=kOutput, calls=%fused_computation.23 | convolution fusion | flops 2957574144 | bytes 15082496 | tf_op jit(solution)/shard_map/dot_general | solution.py:143
  386.4 0.0 reduce-scatter.2.cloned.1.call-update
  386.5 23.1 %reduce-scatter.2.cloned.1.call-done = bf16[256,512]{1,0:T(8,128)(2,1)} async-done(((bf16[256,2048]{1,0:T(8,128)(2,1)}), bf16[256,512]{1,0:T(8,128)(2,1)}) %reduce-scatter.2.cloned.1.call-update) | async-done | bytes 262160 | tf_op jit(solution)/shard_map/reduce_scatter | solution.py:149
  409.5 1.8 fusion.21
  411.4 5.7 %all-reduce = (f32[2,128]{1,0:T(2,128)S(1)}, f32[2,128]{1,0:T(2,128)S(1)}) all-reduce(f32[2,128]{1,0:T(2,128)S(1)} %bitcast.52, f32[2,128]{1,0:T(2,128)S(1)} %bitcast.51), channel_id=1, replica_groups=mesh['seq'=8,'mp'=4] {'mp'}, use_global_device_ids=true, to_apply=%region_9.10 | all-reduce | flops 512 | bytes 4096 | tf_op jit(solution)/shard_map/psum | solution.py:157
  417.1 0.7 fusion.41
  417.8 21.5 %psum.31 = f32[2]{0:T(128)S(1)} all-reduce(f32[2]{0:T(128)S(1)} %get-tuple-element.23), channel_id=1, replica_groups=mesh['seq'=8,'mp'=4] {'seq'}, use_global_device_ids=true, to_apply=%region_13.14 | all-reduce | flops 2 | bytes 16 | tf_op jit(solution)/shard_map/psum | solution.py:163
  439.4 0.5 convert_divide_fusion
  (27 shorter events, 0.1 us)
Async XLA Ops:
  8.0 86.5 %copy-start = (bf16[512,2048]{1,0:T(8,128)(2,1)S(1)}, bf16[512,2048]{1,0:T(8,128)(2,1)}, u32[]{:S(2)}) copy-start(bf16[512,2048]{1,0:T(8,128)(2,1)} %param.24) | copy-start | bytes 6291460
  8.0 126.1 %all-reduce.3.cloned.1.call-start = ((), (), s32[]{:S(2)}) async-start(), calls=%async_computation.1 | async-start | bytes 2097152 | tf_op jit(solution)/shard_map/psum | solution.py:128
  9.8 2.4 copy-start.4
  12.2 38.1 %copy-start.9 = (f32[256]{0:T(256)S(1)}, f32[256]{0:T(256)}, u32[]{:S(2)}) copy-start(f32[256]{0:T(256)} %param.23) | copy-start | bytes 3076
  12.6 72.4 %copy-start.8 = (f32[512]{0:T(512)S(1)}, f32[512]{0:T(512)}, u32[]{:S(2)}) copy-start(f32[512]{0:T(512)} %param.19) | copy-start | bytes 6148
  13.3 71.7 %copy-start.6 = (bf16[2048,512]{1,0:T(8,128)(2,1)S(1)}, bf16[2048,512]{1,0:T(8,128)(2,1)}, u32[]{:S(2)}) copy-start(bf16[2048,512]{1,0:T(8,128)(2,1)} %param.18) | copy-start | bytes 6291460
  87.8 2.6 copy-start.2
  90.5 1.0 copy-start.3
  96.2 38.0 %copy-start.1 = (bf16[2,128,2048]{2,1,0:T(8,128)(2,1)S(1)}, bf16[2,128,2048]{2,1,0:T(8,128)(2,1)}, u32[]{:S(2)}) copy-start(bf16[2,128,2048]{2,1,0:T(8,128)(2,1)} %param.16) | copy-start | bytes 3145732
  96.2 96.0 %all-gather.4.cloned.1.call-start = ((), (), s32[]{:S(2)}) async-start(), calls=%async_computation.2 | async-start | bytes 6488064 | tf_op jit(solution)/shard_map/all_gather | solution.py:134
  96.8 187.8 %all-gather.6.cloned.1.call-start = ((), (), s32[]{:S(2)}) async-start(), calls=%async_computation.3 | async-start | bytes 6488064 | tf_op jit(solution)/shard_map/all_gather | solution.py:139
  97.4 94.9 %copy-start.7 = (f32[2048]{0:T(1024)S(1)}, f32[2048]{0:T(1024)}, u32[]{:S(2)}) copy-start(f32[2048]{0:T(1024)} %param.25) | copy-start | bytes 24580
  97.4 279.5 %all-gather.8.cloned.1.call-start = ((), (), s32[]{:S(2)}) async-start(), calls=%async_computation.4 | async-start | bytes 6488064 | tf_op jit(solution)/shard_map/all_gather | solution.py:145
  97.9 311.6 %reduce-scatter.2.cloned.1.call-start = ((), (), s32[]{:S(2)}) async-start(), calls=%async_computation.5 | async-start | bytes 1310720 | tf_op jit(solution)/shard_map/reduce_scatter | solution.py:149
  386.4 30.7 %copy-start.5 = (s32[2]{0:T(128)S(1)}, s32[2]{0:T(128)}, u32[]{:S(2)}) copy-start(s32[2]{0:T(128)} %param.29) | copy-start | bytes 28
Sparse Core Ops, SparseCore 0:
  96.3 37.7 all-reduce.2
  386.6 22.9 reduce-scatter.1
Sparse Core Ops, SparseCore 1:
  98.9 93.3 all-gather.3
  194.3 90.2 all-gather.5
  286.6 90.2 all-gather.7
where the time goes:
time: 448 us; the launch traced here: 447 us
  waiting for transfers between devices  295 us (66%)
  blocking collectives  95.7 us (21%)
  matrix products  22.6 us (5%)
  between operations  15.9 us (4%)
  other arithmetic  15.5 us (3%)
    all_gather x1, waiting for transfers between devices, local(): lax.all_gather(down_weight, 'seq', axis=0, tiled=True)  92.4 us
    all_gather x1, waiting for transfers between devices, local(): lax.all_gather(up_weight, 'seq', axis=0, tiled=True)  86.4 us
    all_gather x1, waiting for transfers between devices, local(): lax.all_gather(gate_weight, 'seq', axis=0, tiled=True)  55.5 us
    psum x1, waiting for transfers between devices, local(): summed = lax.psum(projected.astype(jnp.bfloat16), 'mp').astype(jnp.float32)  35.9 us
    all_gather x1, blocking collectives, local(): key_piece = lax.all_gather(rotated_k, 'seq', axis=1, tiled=True)  35.3 us
    all_gather x1, blocking collectives, local(): value_piece = lax.all_gather(value_rows, 'seq', axis=1, tiled=True)  33.2 us
    reduce_scatter x1, waiting for transfers between devices, local(): lax.psum_scatter(down_part.astype(jnp.bfloat16), 'mp', scatter_dimension=...  23.1 us
    psum x1, blocking collectives, local(): seq_total = lax.psum(jnp.sum(influence, axis=1), 'seq')  21.5 us
  transfers between devices with their start and end apart: 5, of which 5 were waited for; matrix products, arithmetic and copies ran while one was open for 2% of the time, Pallas kernels for 0%

commit v1 on v0

--- a/solution.py
+++ b/solution.py
@@ -105,7 +105,7 @@
     )
     key_start = jnp.int32(0)
     key_piece = lax.all_gather(rotated_k, "seq", axis=1, tiled=True)
-    value_piece = lax.all_gather(value_rows, "seq", axis=1, tiled=True)
+    value_piece = jnp.concatenate(lax.all_gather(value_rows, "seq"), axis=1)
     updated = []
     for state, query_entry in zip(initial, query_sets):
         queries, first_pos = query_entry

time: 448 us -> 448 us (level)
  no operation moved by 1% of the time
where the time goes in v1:
time: 448 us; the launch traced here: 447 us
  waiting for transfers between devices  295 us (66%)
  blocking collectives  95.7 us (21%)
  matrix products  22.6 us (5%)
  between operations  15.9 us (4%)
  other arithmetic  15.5 us (3%)
    all_gather x1, waiting for transfers between devices, local(): lax.all_gather(down_weight, 'seq', axis=0, tiled=True)  92.4 us
    all_gather x1, waiting for transfers between devices, local(): lax.all_gather(up_weight, 'seq', axis=0, tiled=True)  86.4 us
    all_gather x1, waiting for transfers between devices, local(): lax.all_gather(gate_weight, 'seq', axis=0, tiled=True)  55.5 us
    psum x1, waiting for transfers between devices, local(): summed = lax.psum(projected.astype(jnp.bfloat16), 'mp').astype(jnp.float32)  35.9 us
    all_gather x1, blocking collectives, local(): key_piece = lax.all_gather(rotated_k, 'seq', axis=1, tiled=True)  35.3 us
    all_gather x1, blocking collectives, local(): value_piece = jnp.concatenate(lax.all_gather(value_rows, 'seq'), axis=1)  33.2 us
    reduce_scatter x1, waiting for transfers between devices, local(): lax.psum_scatter(down_part.astype(jnp.bfloat16), 'mp', scatter_dimension=...  23.1 us
    psum x1, blocking collectives, local(): seq_total = lax.psum(jnp.sum(influence, axis=1), 'seq')  21.5 us
  transfers between devices with their start and end apart: 5, of which 5 were waited for; matrix products, arithmetic and copies ran while one was open for 2% of the time, Pallas kernels for 0%

profile of v1, /device:TPU:0, one launch (start us, length us, event | category | flops | bytes accessed | tf_op | source)
XLA Modules:
  0.0 447.5 jit_solution(15365693983427392160)
XLA Ops:
  8.0 0.0 all-reduce.3.cloned.1.call-start
  8.1 1.6 multiply_reduce_fusion
  9.8 0.8 dynamic_slice.19
  10.6 1.5 fusion.13
  12.2 0.4 convolution_add_fusion.2
  12.6 0.7 slice_negate_fusion.1
  13.3 0.1 broadcast_multiply_fusion
  13.4 0.3 fusion.35
  13.8 1.2 fusion.33
  15.0 35.3 %all_gather.15 = bf16[2,1024,128]{2,1,0:T(8,128)(2,1)} all-gather(bf16[2,128,128]{2,1,0:T(8,128)(2,1)S(1)} %fusion.33), channel_id=1, replica_groups=mesh['seq'=8,'mp'=4] {'seq'}, dimensions={1}, use_global_device_ids=true | all-gather | bytes 589824 | tf_op jit(solution)/shard_map/all_gather | solution.py:107
  50.2 0.1 dynamic_slice.21
  50.3 1.5 fusion.18
  51.8 33.2 %all_gather.16 = bf16[8,2,128,128]{3,2,0,1:T(8,128)(2,1)} all-gather(bf16[1,2,128,128]{3,2,0,1:T(8,128)(2,1)S(1)} %bitcast.55), channel_id=1, replica_groups=mesh['seq'=8,'mp'=4] {'seq'}, dimensions={0}, use_global_device_ids=true | all-gather | bytes 589824 | tf_op jit(solution)/shard_map/all_gather | solution.py:108
  85.0 1.5 convolution_add_fusion
  86.5 1.2 reshape.198
  87.8 1.2 slice_negate_fusion
  88.9 1.4 fusion.22
  90.4 3.7 conditional.1
  90.4 0.1 iota_compare_fusion
  90.5 0.9 fusion
  91.5 0.1 copy-done.3
  91.6 1.1 fusion.3
  92.7 1.3 fusion.2
  94.0 0.2 fusion.31
  94.3 0.2 copy.21
  94.5 1.7 convolution_convert_fusion
  96.2 0.0 all-reduce.3.cloned.1.call-update
  96.2 0.0 all-gather.4.cloned.1.call-start
  96.2 0.5 all-gather.4.cloned.1.call-update
  96.8 0.0 all-gather.6.cloned.1.call-start
  96.8 0.5 all-gather.6.cloned.1.call-update
  97.4 0.0 all-gather.8.cloned.1.call-start
  97.4 0.5 all-gather.8.cloned.1.call-update
  97.9 0.2 reduce-scatter.2.cloned.1.call-start
  98.2 35.9 %all-reduce.3.cloned.1.call-done = bf16[256,2048]{1,0:T(8,128)(2,1)} async-done(((bf16[256,2048]{1,0:T(8,128)(2,1)}), bf16[256,2048]{1,0:T(8,128)(2,1)}) %all-reduce.3.cloned.1.call-update) | async-done | bytes 1048592 | tf_op jit(solution)/shard_map/psum | solution.py:128
  134.1 2.6 fusion.15
  136.7 55.5 %all-gather.4.cloned.1.call-done = bf16[2048,1408]{1,0:T(8,128)(2,1)} async-done(((bf16[256,1408]{1,0:T(8,128)(2,1)}), bf16[2048,1408]{1,0:T(8,128)(2,1)}) %all-gather.4.cloned.1.call-update) | async-done | bytes 5767184 | tf_op jit(solution)/shard_map/all_gather | solution.py:134
  192.2 6.0 %fusion.27 = f32[256,1408]{1,0:T(8,128)} fusion(bf16[2048,1408]{1,0:T(8,128)(2,1)} %all-gather.4.cloned.1.call-done, bf16[256,2048]{1,0:T(8,128)(2,1)} %get-tuple-element.28, f32[2048]{0:T(1024)S(1)} %copy-done.7, f32[256]{0:T(256)S(1)} %add_rsqrt_fusion), kind=kOutput, calls=%fused_computation.47 | convolution fusion | flops 1478492160 | bytes 8266752 | tf_op jit(solution)/shard_map/dot_general | solution.py:132
  198.2 86.4 %all-gather.6.cloned.1.call-done = bf16[2048,1408]{1,0:T(8,128)(2,1)} async-done(((bf16[256,1408]{1,0:T(8,128)(2,1)}), bf16[2048,1408]{1,0:T(8,128)(2,1)}) %all-gather.6.cloned.1.call-update) | async-done | bytes 5767184 | tf_op jit(solution)/shard_map/all_gather | solution.py:139
  284.6 92.4 %all-gather.8.cloned.1.call-done = bf16[2048,1408]{1,0:T(8,128)(2,1)} async-done(((bf16[256,1408]{1,0:T(8,128)(2,1)}), bf16[2048,1408]{1,0:T(8,128)(2,1)}) %all-gather.8.cloned.1.call-update) | async-done | bytes 5767184 | tf_op jit(solution)/shard_map/all_gather | solution.py:145
  376.9 9.5 %convolution_convert_fusion.1 = bf16[256,2048]{1,0:T(8,128)(2,1)} fusion(bf16[2048,1408]{1,0:T(8,128)(2,1)} %all-gather.8.cloned.1.call-done, bf16[2048,1408]{1,0:T(8,128)(2,1)} %all-gather.6.cloned.1.call-done, f32[256,1408]{1,0:T(8,128)} %fusion.27, bf16[256,2048]{1,0:T(8,128)(2,1)} %get-tuple-element.28, f32[2048]{0:T(1024)S(1)} %copy-done.7, ...), kind=kOutput, calls=%fused_computation.22 | convolution fusion | flops 2957574144 | bytes 15082496 | tf_op jit(solution)/shard_map/dot_general | solution.py:143
  386.4 0.0 reduce-scatter.2.cloned.1.call-update
  386.5 23.1 %reduce-scatter.2.cloned.1.call-done = bf16[256,512]{1,0:T(8,128)(2,1)} async-done(((bf16[256,2048]{1,0:T(8,128)(2,1)}), bf16[256,512]{1,0:T(8,128)(2,1)}) %reduce-scatter.2.cloned.1.call-update) | async-done | bytes 262160 | tf_op jit(solution)/shard_map/reduce_scatter | solution.py:149
  409.5 1.8 fusion.20
  411.4 5.7 %all-reduce = (f32[2,128]{1,0:T(2,128)S(1)}, f32[2,128]{1,0:T(2,128)S(1)}) all-reduce(f32[2,128]{1,0:T(2,128)S(1)} %bitcast.58, f32[2,128]{1,0:T(2,128)S(1)} %bitcast.57), channel_id=1, replica_groups=mesh['seq'=8,'mp'=4] {'mp'}, use_global_device_ids=true, to_apply=%region_9.10 | all-reduce | flops 512 | bytes 4096 | tf_op jit(solution)/shard_map/psum | solution.py:157
  417.1 0.7 fusion.40
  417.8 21.5 %psum.31 = f32[2]{0:T(128)S(1)} all-reduce(f32[2]{0:T(128)S(1)} %get-tuple-element.24), channel_id=1, replica_groups=mesh['seq'=8,'mp'=4] {'seq'}, use_global_device_ids=true, to_apply=%region_13.14 | all-reduce | flops 2 | bytes 16 | tf_op jit(solution)/shard_map/psum | solution.py:163
  439.4 0.5 convert_divide_fusion
  (27 shorter events, 0.1 us)
Async XLA Ops:
  8.0 86.5 %copy-start = (bf16[512,2048]{1,0:T(8,128)(2,1)S(1)}, bf16[512,2048]{1,0:T(8,128)(2,1)}, u32[]{:S(2)}) copy-start(bf16[512,2048]{1,0:T(8,128)(2,1)} %param.24) | copy-start | bytes 6291460
  8.0 126.1 %all-reduce.3.cloned.1.call-start = ((), (), s32[]{:S(2)}) async-start(), calls=%async_computation.1 | async-start | bytes 2097152 | tf_op jit(solution)/shard_map/psum | solution.py:128
  9.8 2.4 copy-start.4
  12.2 38.1 %copy-start.9 = (f32[256]{0:T(256)S(1)}, f32[256]{0:T(256)}, u32[]{:S(2)}) copy-start(f32[256]{0:T(256)} %param.23) | copy-start | bytes 3076
  12.6 72.4 %copy-start.8 = (f32[512]{0:T(512)S(1)}, f32[512]{0:T(512)}, u32[]{:S(2)}) copy-start(f32[512]{0:T(512)} %param.19) | copy-start | bytes 6148
  13.3 71.7 %copy-start.6 = (bf16[2048,512]{1,0:T(8,128)(2,1)S(1)}, bf16[2048,512]{1,0:T(8,128)(2,1)}, u32[]{:S(2)}) copy-start(bf16[2048,512]{1,0:T(8,128)(2,1)} %param.18) | copy-start | bytes 6291460
  87.8 2.6 copy-start.2
  90.5 1.0 copy-start.3
  96.2 38.0 %copy-start.1 = (bf16[2,128,2048]{2,1,0:T(8,128)(2,1)S(1)}, bf16[2,128,2048]{2,1,0:T(8,128)(2,1)}, u32[]{:S(2)}) copy-start(bf16[2,128,2048]{2,1,0:T(8,128)(2,1)} %param.16) | copy-start | bytes 3145732
  96.2 96.0 %all-gather.4.cloned.1.call-start = ((), (), s32[]{:S(2)}) async-start(), calls=%async_computation.2 | async-start | bytes 6488064 | tf_op jit(solution)/shard_map/all_gather | solution.py:134
  96.8 187.8 %all-gather.6.cloned.1.call-start = ((), (), s32[]{:S(2)}) async-start(), calls=%async_computation.3 | async-start | bytes 6488064 | tf_op jit(solution)/shard_map/all_gather | solution.py:139
  97.4 94.9 %copy-start.7 = (f32[2048]{0:T(1024)S(1)}, f32[2048]{0:T(1024)}, u32[]{:S(2)}) copy-start(f32[2048]{0:T(1024)} %param.25) | copy-start | bytes 24580
  97.4 279.5 %all-gather.8.cloned.1.call-start = ((), (), s32[]{:S(2)}) async-start(), calls=%async_computation.4 | async-start | bytes 6488064 | tf_op jit(solution)/shard_map/all_gather | solution.py:145
  97.9 311.6 %reduce-scatter.2.cloned.1.call-start = ((), (), s32[]{:S(2)}) async-start(), calls=%async_computation.5 | async-start | bytes 1310720 | tf_op jit(solution)/shard_map/reduce_scatter | solution.py:149
  386.4 30.7 %copy-start.5 = (s32[2]{0:T(128)S(1)}, s32[2]{0:T(128)}, u32[]{:S(2)}) copy-start(s32[2]{0:T(128)} %param.29) | copy-start | bytes 28
Sparse Core Ops, SparseCore 0:
  96.3 37.7 all-reduce.2
  386.6 22.9 reduce-scatter.1
Sparse Core Ops, SparseCore 1:
  98.9 93.3 all-gather.3
  194.3 90.2 all-gather.5
  286.6 90.2 all-gather.7
